TPU v7x, 32 devices: a whole 2x2x4 slice. The times are simulated.
32 devices in a mesh: grp: 2 (over y), depth: 4 (over x, core), shot: 4 (over z).
Axes of the slice: x: 2, y: 2, z: 4, core: 2. Of those that a mesh axis runs over, the one named last changes fastest.
Arguments:
- forward: bfloat16 [4, 8, 32, 32, 128], P(None, ('grp', 'shot'), 'depth'), parts along dimension 1, may hold values from -6 to 6
- adjoint_last: float32 [8, 32, 32, 128], P(('grp', 'shot'), 'depth'), parts along dimension 0, may hold values from -6 to 6
- adjoint_late: float32 [8, 32, 32, 128], P(('grp', 'shot'), 'depth'), parts along dimension 0, may hold values from -6 to 6
- residuals: float32 [8, 4, 256], P(('grp', 'shot')), parts along dimension 0, may hold values from -6 to 6
- source_cells: int32 [8, 3], P('grp'), parts along dimension 0, may hold values from 0 to 127, as said below
- receiver_cells: int32 [8, 256, 3], P('grp'), parts along dimension 0, may hold values from 0 to 127, as said below
- assignment: int32 [8], P('grp'), parts along dimension 0, may hold values from 0 to 3, each once
- model: float32 [6, 32, 16, 64], P(None, ('grp', 'depth'), 'shot'), parts along dimension 1, may hold values from -0.4 to 2, as said below
Outputs:
- adjoint_first: float32 [8, 32, 32, 128], P(('grp', 'shot'), 'depth'), parts along dimension 0
- gradients: float32 [6, 32, 16, 64], P(None, ('grp', 'depth'), 'shot'), parts along dimension 1
There are 2 independent parts, one for each index of `grp`. A program takes and returns all parts, laid end to end along the dimension named above; each array names one. Nothing has to cross between parts.
Inputs may be any that keep to these rules, and one draw needn't show every extreme that they name: `source_cells`: each row holds the depth, second and third cell index of a source inside the grid of 32 x 32 x 128 cells. `receiver_cells`: each entry holds the depth, second and third cell index of a receiver inside the grid; receivers may share a cell. `assignment`: each survey row is used by exactly one shot. `model`: channel 0 (depth with depth) lies in 1 to 2; channels 1 and 2 (second with second, third with third) lie in 0.25 to 1; channels 3 to 5 (depth with second, depth with third, second with third) lie in -0.4 to 0.4.
All inputs are finite; a program needn't handle non-finite values.
Results may differ from a plain program's by a relative error of at most 0.0003.
Values sent between devices are 32-bit elements; how exact they have to be, the bound alone decides.
A program may use at most 128 MiB of HBM per device.

v0:
```python
import jax
import jax.numpy as jnp
from jax import lax
from jax.sharding import PartitionSpec as P

MUTE = 3


TIME_SQUARED = 0.2


def extended_2(array, sides, width):
    for axis, dim in sides:
        devices, length = (lax.axis_size(axis), array.shape[dim])
        up = [(i, (i + 1) % devices) for i in range(devices - 1)]
        down = [(j, i) for i, j in up]
        last = lax.slice_in_dim(array, length - width, length, axis=dim)
        leading = lax.slice_in_dim(array, 0, width, axis=dim)
        before = lax.ppermute(last, axis, up)
        after = lax.ppermute(leading, axis, down)
        array = jnp.concatenate([before, array, after], axis=dim)
    return array


def passed_along(array, axis, by):
    devices = lax.axis_size(axis)
    pairs = [(i, i + by) for i in range(devices) if 0 <= i + by < devices]
    return lax.ppermute(array, axis, pairs)


def refine(coarse, dimension):
    coarse_count = coarse.shape[dimension]
    later_rows = lax.slice_in_dim(coarse, 1, coarse_count, axis=dimension)
    edge_row = lax.slice_in_dim(coarse, coarse_count - 1, coarse_count, axis=dimension)
    middle = (coarse + jnp.concatenate([later_rows, edge_row], axis=dimension)) * 0.5
    merged = jnp.stack([coarse, middle], axis=dimension + 1)
    new_shape = coarse.shape[:dimension] + (2 * coarse_count,) + coarse.shape[dimension + 1 :]
    return merged.reshape(new_shape)


def coarsen(fine_cells, dimension):
    half_count = fine_cells.shape[dimension] // 2
    paired = fine_cells.reshape(
        fine_cells.shape[:dimension] + (half_count, 2) + fine_cells.shape[dimension + 1 :]
    )
    even_cells = lax.index_in_dim(paired, 0, dimension + 1, keepdims=False)
    odd_cells = lax.index_in_dim(paired, 1, dimension + 1, keepdims=False)
    first_odd = lax.slice_in_dim(odd_cells, 0, 1, axis=dimension)
    earlier = jnp.concatenate(
        [jnp.zeros_like(first_odd), lax.slice_in_dim(odd_cells, 0, half_count - 1, axis=dimension)],
        axis=dimension,
    )
    tail_part = jnp.concatenate(
        [
            jnp.zeros_like(lax.slice_in_dim(odd_cells, 1, half_count, axis=dimension)),
            lax.slice_in_dim(odd_cells, half_count - 1, half_count, axis=dimension),
        ],
        axis=dimension,
    )
    return even_cells + 0.5 * odd_cells + 0.5 * earlier + 0.5 * tail_part


def coarsen_depth(fine_cells, rim_layer, last_scale):
    half_count = fine_cells.shape[1] // 2
    paired = fine_cells.reshape((fine_cells.shape[0], half_count, 2) + fine_cells.shape[2:])
    even_cells = paired[:, :, 0]
    odd_cells = paired[:, :, 1]
    earlier = jnp.concatenate([rim_layer, odd_cells[:, : half_count - 1]], axis=1)
    tail_part = jnp.concatenate(
        [jnp.zeros_like(odd_cells[:, 1:]), odd_cells[:, half_count - 1 :]], axis=1
    )
    return even_cells + 0.5 * odd_cells + 0.5 * earlier + last_scale * tail_part


def window(padded, offsets):
    depth_step, row_step, column_step = offsets
    inner_depth = padded.shape[-3] - 2
    inner_rows = padded.shape[-2] - 2
    inner_columns = padded.shape[-1] - 2
    return padded[
        ...,
        1 + depth_step : 1 + depth_step + inner_depth,
        1 + row_step : 1 + row_step + inner_rows,
        1 + column_step : 1 + column_step + inner_columns,
    ]


def derivatives(padded):
    centre = window(padded, (0, 0, 0))

    def second(offsets, opposite):
        return window(padded, offsets) - 2.0 * centre + window(padded, opposite)

    def cross(upper_one, upper_two, lower_one, lower_two):
        return (
            window(padded, upper_one)
            - window(padded, upper_two)
            - window(padded, lower_one)
            + window(padded, lower_two)
        ) * 0.25

    return jnp.stack(
        [
            second((1, 0, 0), (-1, 0, 0)),
            second((0, 1, 0), (0, -1, 0)),
            second((0, 0, 1), (0, 0, -1)),
            cross((1, 1, 0), (1, -1, 0), (-1, 1, 0), (-1, -1, 0)),
            cross((1, 0, 1), (1, 0, -1), (-1, 0, 1), (-1, 0, -1)),
            cross((0, 1, 1), (0, 1, -1), (0, -1, 1), (0, -1, -1)),
        ],
        axis=0,
    )


def side_pad(wave_field):
    return jnp.pad(wave_field, ((0, 0), (0, 0), (1, 1), (1, 1)))


def inject(wave_field, receivers, values, depth_first):
    shots_here, depth_len, row_len, column_len = wave_field.shape
    local_depth = receivers[..., 0] - depth_first
    inside = (local_depth >= 0) & (local_depth < depth_len)
    shot_rows = jnp.arange(shots_here, dtype=jnp.int32)[:, None]
    flat_index = (
        (shot_rows * depth_len + local_depth) * row_len + receivers[..., 1]
    ) * column_len + receivers[..., 2]
    flat_index = jnp.where(inside, flat_index, wave_field.size)
    added = wave_field.reshape(-1).at[flat_index.reshape(-1)].add(values.reshape(-1), mode="drop")
    return added.reshape(wave_field.shape)


def on_device(
    forward, adjoint_last, adjoint_late, residuals, source_cells, receiver_cells, assignment, model
):
    steps_total = forward.shape[0]
    shots_here, depth_len, row_len, column_len = adjoint_last.shape
    depth_index = lax.axis_index("depth")
    depth_count = lax.axis_size("depth")
    last_depth = depth_index == depth_count - 1
    last_scale = jnp.where(last_depth, 0.5, 0.0).astype(jnp.float32)
    depth_first = depth_index * depth_len
    current, previous = (adjoint_last, adjoint_late)
    reach = steps_total // 2 + 1
    coarse_total = depth_count * depth_len // 2
    fine_total = depth_count * depth_len
    coarse_first = depth_index * (depth_len // 2) - reach
    fine_offset = 2 * reach - steps_total
    fine_count = depth_len + 2 * steps_total
    extended = extended_2(model, (("depth", 1),), reach)
    piece = lax.all_gather(extended, "shot", axis=2, tiled=True)
    count = piece.shape[1]
    global_rows = coarse_first + jnp.arange(count, dtype=jnp.int32)
    later_rows = jnp.concatenate([piece[:, 1:], jnp.zeros_like(piece[:, :1])], axis=1)
    following = jnp.where((global_rows == coarse_total - 1)[None, :, None, None], piece, later_rows)
    middle = (piece + following) * 0.5
    deeper = jnp.stack([piece, middle], axis=2).reshape(
        (piece.shape[0], 2 * count) + piece.shape[2:]
    )
    sliced = deeper[:, fine_offset : fine_offset + fine_count]
    fine_rows = 2 * coarse_first + fine_offset + jnp.arange(fine_count, dtype=jnp.int32)
    inside = (fine_rows >= 0) & (fine_rows < fine_total)
    sliced = jnp.where(inside[None, :, None, None], sliced, jnp.zeros_like(sliced))
    gathered = refine(sliced, 3)
    used_coefficients = refine(gathered, 2)
    both_fields = extended_2(jnp.stack([current, previous]), (("depth", 2),), steps_total)
    current, previous = (both_fields[0], both_fields[1])
    survey_count = assignment.shape[0]
    survey_ids = jnp.arange(survey_count, dtype=jnp.int32)
    shot_ids = lax.axis_index("shot") * shots_here + jnp.arange(shots_here, dtype=jnp.int32)
    geometry = jnp.sum(
        jnp.where(survey_ids[None, :] == shot_ids[:, None], assignment[None, :], 0), axis=1
    )
    chosen = survey_ids[None, :] == geometry[:, None]
    sources = jnp.sum(jnp.where(chosen[:, :, None], source_cells[None], 0), axis=1)
    receivers = jnp.sum(jnp.where(chosen[:, :, None, None], receiver_cells[None], 0), axis=1)
    depth_cells = depth_first + jnp.arange(depth_len, dtype=jnp.int32)
    row_cells = jnp.arange(row_len, dtype=jnp.int32)
    column_cells = jnp.arange(column_len, dtype=jnp.int32)
    muted = (
        (jnp.abs(depth_cells[None, :] - sources[:, 0:1]) <= MUTE)[:, :, None, None]
        & (jnp.abs(row_cells[None, :] - sources[:, 1:2]) <= MUTE)[:, None, :, None]
        & (jnp.abs(column_cells[None, :] - sources[:, 2:3]) <= MUTE)[:, None, None, :]
    )
    totals = jnp.zeros((6, shots_here, depth_len, row_len, column_len), jnp.float32)
    for step_index in range(steps_total):
        slopes = derivatives(side_pad(jnp.pad(current, ((0, 0), (1, 1), (0, 0), (0, 0)))))
        owned_slopes = slopes[:, :, steps_total : steps_total + depth_len]
        term = forward[step_index].astype(jnp.float32)[None] * owned_slopes
        totals = totals + term
        updated = (
            2.0 * current
            - previous
            + TIME_SQUARED * jnp.sum(used_coefficients[:, None] * slopes, axis=0)
        )
        updated = inject(updated, receivers, residuals[:, step_index], depth_first - steps_total)
        previous, current = (current, updated)
    kept = jnp.sum(jnp.where(muted[None], jnp.zeros_like(totals), totals), axis=1)
    coarse_rows = coarsen(coarsen(kept, 3), 2)
    rim_layer = passed_along(coarse_rows[:, depth_len - 1 :], "depth", 1)
    gradients = lax.psum_scatter(
        coarsen_depth(coarse_rows, rim_layer, last_scale), "shot", scatter_dimension=2, tiled=True
    )
    adjoint_first = current[:, steps_total : steps_total + depth_len]
    return (adjoint_first, gradients / steps_total)


def solution(mesh):
    placed = (
        P(None, ("grp", "shot"), "depth", None, None),
        P(("grp", "shot"), "depth", None, None),
        P(("grp", "shot"), "depth", None, None),
        P(("grp", "shot"), None, None),
        P("grp", None),
        P("grp", None, None),
        P("grp"),
        P(None, ("grp", "depth"), "shot", None),
    )
    return jax.shard_map(
        on_device,
        mesh=mesh,
        in_specs=placed,
        out_specs=(
            P(("grp", "shot"), "depth", None, None),
            P(None, ("grp", "depth"), "shot", None),
        ),
        check_vma=False,
    )
```

profile of v0, /device:TPU:0, one launch (start us, length us, event | category | flops | bytes accessed | tf_op | source)
XLA Modules:
  0.0 177.3 jit_solution(18199098292120019333)
XLA Ops:
  8.1 2.4 %collective-permute-start.2 = (f32[6,3,4,64]{3,0,1,2:T(8,128)S(1)}, f32[6,3,4,64]{3,0,1,2:T(8,128)S(1)}, u32[]{:S(2)}, u32[]{:S(2)}) collective-permute-start(f32[6,3,4,64]{3,0,1,2:T(8,128)S(1)} %get-tuple-element.59), channel_id=1, source_target_pairs={{0,4},{4,8},{8,12},{1,5},{5,9},{9,13},{2,6},{6,10},{10,14},{3,7},{... | collective-permute-start | bytes 55304 | tf_op jit(solution)/shard_map/ppermute | solution.py:19
  12.7 5.1 %collective-permute-start = (f32[2,1,4,32,128]{4,3,2,1,0:T(8,128)S(1)}, f32[2,1,4,32,128]{4,3,2,1,0:T(8,128)S(1)}, u32[]{:S(2)}, u32[]{:S(2)}) collective-permute-start(f32[2,1,4,32,128]{4,3,2,1,0:T(8,128)S(1)} %get-tuple-element.57), channel_id=1, source_target_pairs={{0,4},{4,8},{8,12},{1,5},{5,9},{9,13},{2,6},{6,10},{10,14},{3,7},{... | collective-permute-start | bytes 393224 | tf_op jit(solution)/shard_map/ppermute | solution.py:19
  26.1 1.7 bitcast_convert_fusion.3
  29.9 17.3 %all_gather.3 = f32[6,10,16,64]{3,0,1,2:T(8,128)S(1)} all-gather(f32[6,10,4,64]{3,0,1,2:T(8,128)S(1)} %pad_maximum_fusion.4), channel_id=1, replica_groups=mesh['grp'=2,'depth'=4,'shot'=4] {'shot'}, dimensions={2}, use_global_device_ids=true | all-gather | bytes 307200 | tf_op jit(solution)/shard_map/all_gather | solution.py:150
  49.0 6.1 %copy.380 = f32[6,16,16,64,2]{2,1,4,3,0:T(8,128)} copy(f32[6,16,16,64,2]{3,2,1,0,4:T(8,128)S(1)} %pad_maximum_fusion) | data formatting | bytes 1572864 | tf_op jit(solution)/shard_map/stack | solution.py:36
  55.2 7.2 %slice.500 = f32[6,16,1,128]{2,1,3,0:T(8,128)} slice(f32[6,16,16,128]{2,1,3,0:T(8,128)} %bitcast.178), slice={[0:6], [0:16], [15:16], [0:128]} | slice | bytes 98304 | tf_op jit(solution)/shard_map/slice | solution.py:34
  62.4 4.3 %slice_bitcast_fusion = f32[6,16,15,1,128]{2,1,4,0,3:T(8,128)} fusion(f32[6,16,16,128]{2,1,3,0:T(8,128)S(1)} %bitcast.181), kind=kLoop, calls=%fused_computation.4 | loop fusion | bytes 1474560 | tf_op jit(solution)/shard_map/concatenate | solution.py:35
  66.7 4.7 %copy.382 = f32[6,16,1,128]{3,1,0,2:T(8,128)S(1)} copy(f32[6,16,1,128]{2,1,3,0:T(8,128)} %slice.500) | data formatting | bytes 98304 | tf_op jit(solution)/shard_map/slice | solution.py:34
  71.4 4.2 %copy.383 = f32[6,16,1,1,128]{2,1,4,0,3:T(8,128)} copy(f32[6,16,1,1,128]{4,1,0,3,2:T(8,128)S(1)} %bitcast.240) | data formatting | bytes 98304 | tf_op jit(solution)/shard_map/concatenate | solution.py:35
  75.6 10.7 %fusion = f32[6,16,16,1,128]{2,1,4,0,3:T(8,128)} fusion(f32[6,16,16,1,128]{2,1,4,0,3:T(8,128)} %bitcast.179, f32[6,16,1,1,128]{2,1,4,0,3:T(8,128)} %copy.383, f32[6,16,15,1,128]{2,1,4,0,3:T(8,128)} %slice_bitcast_fusion), kind=kLoop, calls=%fused_computation.6 | loop fusion | flops 589824 | bytes 2359296 | tf_op jit(solution)/shard_map/mul | solution.py:35
  86.3 4.6 %copy.384 = f32[6,16,16,1,128]{4,2,3,1,0:T(8,128)S(1)} copy(f32[6,16,16,1,128]{2,1,4,0,3:T(8,128)} %bitcast.180) | data formatting | bytes 1572864 | tf_op jit(solution)/shard_map/stack;reshape | solution.py:36
  90.9 4.7 %copy.385 = f32[6,16,16,1,128]{4,2,3,1,0:T(8,128)S(1)} copy(f32[6,16,16,1,128]{2,1,4,0,3:T(8,128)} %fusion) | data formatting | bytes 1572864 | tf_op jit(solution)/shard_map/mul | solution.py:35
  98.5 2.3 %scatter_fusion = f32[65536]{0:T(1024)S(1)} fusion(f32[65536]{0:T(1024)S(1)} %subtract_add_fusion.3, s32[256]{0:T(256)S(1)} %bitcast.242, f32[256]{0:T(256)S(1)} %bitcast.251), kind=kCustom, calls=%fused_computation | custom fusion | flops 256 | bytes 4096 | tf_op jit(solution)/shard_map/scatter-add | solution.py:128
  103.7 2.1 %scatter_fusion.1 = f32[65536]{0:T(1024)S(1)} fusion(f32[65536]{0:T(1024)S(1)} %subtract_add_fusion.2, s32[256]{0:T(256)S(1)} %bitcast.243, f32[256]{0:T(256)S(1)} %bitcast.250), kind=kCustom, calls=%fused_computation.1 | custom fusion | flops 256 | bytes 4096 | tf_op jit(solution)/shard_map/scatter-add | solution.py:128
  108.6 2.1 %scatter_fusion.2 = f32[65536]{0:T(1024)S(1)} fusion(f32[65536]{0:T(1024)S(1)} %subtract_add_fusion.1, s32[256]{0:T(256)S(1)} %bitcast.244, f32[256]{0:T(256)S(1)} %bitcast.249), kind=kCustom, calls=%fused_computation.2 | custom fusion | flops 256 | bytes 4096 | tf_op jit(solution)/shard_map/scatter-add | solution.py:128
  115.2 2.2 %copy.446 = f32[6,1,8,32,128]{3,2,4,0,1:T(8,128)} copy(f32[6,1,8,32,128]{4,3,2,1,0:T(8,128)S(1)} %fusion.5) | data formatting | bytes 1572864 | tf_op jit(solution)/shard_map/jit(_where)/select_n | solution.py:197
  117.4 1.5 slice_bitcast_fusion.1
  119.0 1.8 copy-done.1
  120.8 1.4 fusion.3
  122.2 1.9 %copy.451 = f32[6,8,32,64]{3,1,2,0:T(8,128)S(1)} copy(f32[6,8,32,64]{2,1,3,0:T(8,128)} %fusion.3) | data formatting | bytes 786432 | tf_op jit(solution)/shard_map/add | solution.py:60
  124.4 3.0 %collective-permute-start.4 = (f32[6,1,16,64]{3,1,2,0:T(1,128)S(1)}, f32[6,1,16,64]{3,1,2,0:T(1,128)S(1)}, u32[]{:S(2)}, u32[]{:S(2)}) collective-permute-start(f32[6,1,16,64]{3,1,2,0:T(1,128)S(1)} %slice.519), channel_id=1, source_target_pairs={{0,4},{4,8},{8,12},{1,5},{5,9},{9,13},{2,6},{6,10},{10,14},{3,7},{... | collective-permute-start | bytes 73736 | tf_op jit(solution)/shard_map/ppermute | solution.py:28
  129.1 2.1 %scatter_fusion.3 = f32[65536]{0:T(1024)S(1)} fusion(f32[65536]{0:T(1024)S(1)} %subtract_add_fusion, s32[256]{0:T(256)S(1)} %bitcast.245, f32[256]{0:T(256)S(1)} %bitcast.248), kind=kCustom, calls=%fused_computation.3 | custom fusion | flops 256 | bytes 4096 | tf_op jit(solution)/shard_map/scatter-add | solution.py:128
  131.9 37.1 %all-reduce.17.cloned.1.call-done = f32[6,4,16,64]{3,2,1,0:T(8,128)} async-done(((f32[6,4,16,64]{3,2,1,0:T(8,128)}), f32[6,4,16,64]{3,2,1,0:T(8,128)}) %all-reduce.17.cloned.1.call-update) | async-done | bytes 98320
  169.0 1.5 dynamic-slice_multiply_fusion
  (160 shorter events, 29.8 us)
Async XLA Ops:
  7.2 21.4 %copy-start.18 = (u32[32]{0:T(128)S(1)}, u32[32]{0:T(128)}, u32[]{:S(2)}) copy-start(u32[32]{0:T(128)} %constant.101) | copy-start | bytes 388
  7.2 161.8 %all-reduce.17.cloned.1.call-start = ((), (), s32[]{:S(2)}) async-start(), calls=%async_computation | async-start | bytes 393216
  8.1 21.8 %collective-permute-start.2 = (f32[6,3,4,64]{3,0,1,2:T(8,128)S(1)}, f32[6,3,4,64]{3,0,1,2:T(8,128)S(1)}, u32[]{:S(2)}, u32[]{:S(2)}) collective-permute-start(f32[6,3,4,64]{3,0,1,2:T(8,128)S(1)} %get-tuple-element.59), channel_id=1, source_target_pairs={{0,4},{4,8},{8,12},{1,5},{5,9},{9,13},{2,6},{6,10},{10,14},{3,7},{... | collective-permute-start | bytes 55304 | tf_op jit(solution)/shard_map/ppermute | solution.py:19
  10.5 19.4 %collective-permute-start.3 = (f32[6,3,4,64]{3,0,1,2:T(8,128)S(1)}, f32[6,3,4,64]{3,0,1,2:T(8,128)S(1)}, u32[]{:S(2)}, u32[]{:S(2)}) collective-permute-start(f32[6,3,4,64]{3,0,1,2:T(8,128)S(1)} %get-tuple-element.60), channel_id=1, source_target_pairs={{4,0},{8,4},{12,8},{5,1},{9,5},{13,9},{6,2},{10,6},{14,10},{7,3},{... | collective-permute-start | bytes 55304 | tf_op jit(solution)/shard_map/ppermute | solution.py:20
  12.7 82.8 %collective-permute-start = (f32[2,1,4,32,128]{4,3,2,1,0:T(8,128)S(1)}, f32[2,1,4,32,128]{4,3,2,1,0:T(8,128)S(1)}, u32[]{:S(2)}, u32[]{:S(2)}) collective-permute-start(f32[2,1,4,32,128]{4,3,2,1,0:T(8,128)S(1)} %get-tuple-element.57), channel_id=1, source_target_pairs={{0,4},{4,8},{8,12},{1,5},{5,9},{9,13},{2,6},{6,10},{10,14},{3,7},{... | collective-permute-start | bytes 393224 | tf_op jit(solution)/shard_map/ppermute | solution.py:19
  17.9 77.7 %collective-permute-start.1 = (f32[2,1,4,32,128]{4,3,2,1,0:T(8,128)S(1)}, f32[2,1,4,32,128]{4,3,2,1,0:T(8,128)S(1)}, u32[]{:S(2)}, u32[]{:S(2)}) collective-permute-start(f32[2,1,4,32,128]{4,3,2,1,0:T(8,128)S(1)} %get-tuple-element.58), channel_id=1, source_target_pairs={{4,0},{8,4},{12,8},{5,1},{9,5},{13,9},{6,2},{10,6},{14,10},{7,3},{... | collective-permute-start | bytes 393224 | tf_op jit(solution)/shard_map/ppermute | solution.py:20
  55.2 7.2 %copy-start = (f32[6,16,16,64,2]{2,1,4,3,0:T(8,128)S(1)}, f32[6,16,16,64,2]{2,1,4,3,0:T(8,128)}, u32[]{:S(2)}) copy-start(f32[6,16,16,64,2]{2,1,4,3,0:T(8,128)} %copy.380) | copy-start | bytes 2359300
  90.9 4.7 %copy-start.15 = (f32[1,8,32,128]{3,2,1,0:T(8,128)S(1)}, f32[1,8,32,128]{3,2,1,0:T(8,128)}, u32[]{:S(2)}) copy-start(f32[1,8,32,128]{3,2,1,0:T(8,128)} %param.9) | copy-start | bytes 393220
  90.9 4.7 %copy-start.16 = (f32[1,8,32,128]{3,2,1,0:T(8,128)S(1)}, f32[1,8,32,128]{3,2,1,0:T(8,128)}, u32[]{:S(2)}) copy-start(f32[1,8,32,128]{3,2,1,0:T(8,128)} %param.10) | copy-start | bytes 393220
  96.9 1.2 copy-start.10
  106.9 1.2 copy-start.8
  110.8 3.9 %copy-start.11 = (f32[6,1,16,32,128]{4,3,2,1,0:T(8,128)S(1)}, f32[6,1,16,32,128]{4,3,2,1,0:T(8,128)}, u32[]{:S(2)}) copy-start(f32[6,1,16,32,128]{4,3,2,1,0:T(8,128)} %copy-done.10) | copy-start | bytes 4718596
  110.8 3.9 %copy-start.17 = (pred[8,32,128]{2,1,0:T(8,128)(4,1)S(1)}, pred[8,32,128]{2,1,0:T(8,128)(4,1)}, u32[]{:S(2)}) copy-start(pred[8,32,128]{2,1,0:T(8,128)(4,1)} %broadcast_and_fusion) | copy-start | bytes 98308
  111.6 3.1 %copy-start.7 = (f32[6,1,16,32,128]{4,3,2,1,0:T(8,128)S(1)}, f32[6,1,16,32,128]{4,3,2,1,0:T(8,128)}, u32[]{:S(2)}) copy-start(f32[6,1,16,32,128]{4,3,2,1,0:T(8,128)} %copy-done.6) | copy-start | bytes 4718596
  111.6 3.1 %copy-start.9 = (f32[6,1,16,32,128]{4,3,2,1,0:T(8,128)S(1)}, f32[6,1,16,32,128]{4,3,2,1,0:T(8,128)}, u32[]{:S(2)}) copy-start(f32[6,1,16,32,128]{4,3,2,1,0:T(8,128)} %copy-done.8) | copy-start | bytes 4718596
  111.6 3.1 %copy-start.12 = (f32[8,32,128]{2,1,0:T(8,128)S(1)}, f32[8,32,128]{2,1,0:T(8,128)}, u32[]{:S(2)}) copy-start(f32[8,32,128]{2,1,0:T(8,128)} %get-tuple-element.54) | copy-start | bytes 393220
  111.6 3.1 %copy-start.13 = (f32[8,32,128]{2,1,0:T(8,128)S(1)}, f32[8,32,128]{2,1,0:T(8,128)}, u32[]{:S(2)}) copy-start(f32[8,32,128]{2,1,0:T(8,128)} %get-tuple-element.55) | copy-start | bytes 393220
  111.6 3.1 %copy-start.14 = (f32[8,32,128]{2,1,0:T(8,128)S(1)}, f32[8,32,128]{2,1,0:T(8,128)}, u32[]{:S(2)}) copy-start(f32[8,32,128]{2,1,0:T(8,128)} %get-tuple-element.56) | copy-start | bytes 393220
  118.9 1.9 %copy-start.1 = (f32[6,1,8,32,128]{3,2,4,0,1:T(8,128)S(1)}, f32[6,1,8,32,128]{3,2,4,0,1:T(8,128)}, u32[]{:S(2)}) copy-start(f32[6,1,8,32,128]{3,2,4,0,1:T(8,128)} %copy.446) | copy-start | bytes 2359300
  124.2 3.3 %copy-start.4 = (f32[1,16,32,128]{3,2,1,0:T(8,128)S(1)}, f32[1,16,32,128]{3,2,1,0:T(8,128)}, u32[]{:S(2)}) copy-start(f32[1,16,32,128]{3,2,1,0:T(8,128)} %get-tuple-element.47) | copy-start | bytes 786436
  124.2 3.4 %copy-start.5 = (f32[1,16,32,128]{3,2,1,0:T(8,128)S(1)}, f32[1,16,32,128]{3,2,1,0:T(8,128)}, u32[]{:S(2)}) copy-start(f32[1,16,32,128]{3,2,1,0:T(8,128)} %get-tuple-element.45) | copy-start | bytes 786436
  124.3 3.3 %copy-start.2 = (f32[1,16,32,128]{3,2,1,0:T(8,128)S(1)}, f32[1,16,32,128]{3,2,1,0:T(8,128)}, u32[]{:S(2)}) copy-start(f32[1,16,32,128]{3,2,1,0:T(8,128)} %get-tuple-element.41) | copy-start | bytes 786436
  124.3 3.4 %copy-start.3 = (f32[1,16,32,128]{3,2,1,0:T(8,128)S(1)}, f32[1,16,32,128]{3,2,1,0:T(8,128)}, u32[]{:S(2)}) copy-start(f32[1,16,32,128]{3,2,1,0:T(8,128)} %get-tuple-element.39) | copy-start | bytes 786436
  124.4 3.9 %collective-permute-start.4 = (f32[6,1,16,64]{3,1,2,0:T(1,128)S(1)}, f32[6,1,16,64]{3,1,2,0:T(1,128)S(1)}, u32[]{:S(2)}, u32[]{:S(2)}) collective-permute-start(f32[6,1,16,64]{3,1,2,0:T(1,128)S(1)} %slice.519), channel_id=1, source_target_pairs={{0,4},{4,8},{8,12},{1,5},{5,9},{9,13},{2,6},{6,10},{10,14},{3,7},{... | collective-permute-start | bytes 73736 | tf_op jit(solution)/shard_map/ppermute | solution.py:28
  (1 other events, 1.1 us)
Sparse Core Ops, SparseCore 0:
  129.2 39.6 all-reduce.16
where the time goes:
time: 178 us; the launch traced here: 177 us
  local copies, waits for them, and re-layouts  52.1 us (29%)
  other arithmetic  41.9 us (24%)
  waiting for transfers between devices  37.2 us (21%)
  blocking collectives  17.3 us (10%)
  between operations  15.6 us (9%)
  starting transfers between devices  13.2 us (7%)
    unnamed x2, waiting for transfers between devices  37.1 us
    all_gather x1, blocking collectives, on_device(): piece = lax.all_gather(extended, 'shot', axis=2, tiled=True)  17.3 us
    slice x3, local copies, waits for them, and re-layouts, refine(): lax.slice_in_dim(coarse, coarse_count - 1, coarse_count, axis=dimension)  12.2 us
    another operation x2, local copies, waits for them, and re-layouts, refine(): merged = jnp.stack([coarse, middle], axis=dimension + 1)  10.8 us
    mul x1, other arithmetic, refine(): (coarse + jnp.concatenate([later_rows, edge_row], axis=dimension)) * 0.5  10.7 us
    scatter-add x4, other arithmetic, inject(): wave_field.reshape(-1).at[flat_index.reshape(-1)]  8.5 us
    concatenate x2, local copies, waits for them, and re-layouts, refine(): jnp.concatenate([later_rows, edge_row], axis=dimension)  8.48 us
    ppermute x2, starting transfers between devices, extended_2(): before = lax.ppermute(last, axis, up)  7.53 us
  transfers between devices with their start and end apart: 6, of which 2 were waited for; matrix products, arithmetic and copies ran while one was open for 35% of the time, Pallas kernels for 0%

commit v1 on v0

v1 whole, which is shorter than its diff:
```python
import functools

import jax
import jax.numpy as jnp
from jax import lax
from jax.experimental import pallas as pl
from jax.experimental.pallas import tpu as pltpu
from jax.sharding import PartitionSpec as P

MUTE = 3
TIME_SQUARED = 0.2
MESH = pl.DeviceIdType.MESH
F32 = jnp.float32
BF16 = jnp.bfloat16


def split_dot(exact, values, contract):
    high = values.astype(BF16)
    low = (values - high.astype(F32)).astype(BF16)
    return exact_dot(exact, high, contract) + exact_dot(exact, low, contract)


def exact_dot(exact, part, contract):
    if contract == "values_left":
        return lax.dot_general(part, exact, (((1,), (0,)), ((), ())), preferred_element_type=F32)
    return lax.dot_general(exact, part, (((1,), (1,)), ((), ())), preferred_element_type=F32)


def kernel(
    forward, last, late, residuals, receivers, model, assignment, sources,
    adjoint_first, gradients,
    gbuf, coarse_y, fine_x, coef, field_a, field_b, inj, totals, restr, lhs_main, lhs_rim,
    send_main, send_rim, recv_main, recv_rim, total,
    gs_sem, gr_sem, hs_sem, hr_sem, fs_sem, fr_sem, ms_sem, mr_sem, rs_sem, rr_sem,
):
    steps = forward.shape[0]
    depth_len, rows, cols = last.shape[1:]
    coarse_len, rl, half_cols = model.shape[1:]
    shots = lax.axis_size("shot")
    depths = lax.axis_size("depth")
    me = lax.axis_index("shot")
    d = lax.axis_index("depth")
    has_up = d > 0
    has_down = d < depths - 1
    halo = steps
    reach = steps - 1
    window = depth_len + 2 * reach
    coarse_rows = shots * rl

    barrier = pltpu.get_barrier_semaphore()

    def greet(device):
        pl.semaphore_signal(barrier, inc=1, device_id=device, device_id_type=MESH)

    for o in range(1, shots):
        greet({"shot": lax.rem(me + o, shots)})

    @pl.when(has_up)
    def _():
        for o in range(shots):
            greet({"depth": d - 1, "shot": lax.rem(me + o, shots)})

    @pl.when(has_down)
    def _():
        for o in range(shots):
            greet({"depth": d + 1, "shot": lax.rem(me + o, shots)})

    for l in range(coarse_len):
        for c in range(3):
            pair = jnp.concatenate([model[c, l], model[c + 3, l]], axis=-1)
            first = ((l % 2) * 3 + c) * rl
            gbuf[me, 1 + l // 2, first:first + rl, :] = pair

    beside = jnp.where(has_up, shots, 0) + jnp.where(has_down, shots, 0)
    pl.semaphore_wait(barrier, shots - 1 + beside)

    def gather_copy(o, sending):
        peer = lax.rem(me + o, shots) if sending else lax.rem(me + shots - o, shots)
        slot = me if sending else peer
        return pltpu.make_async_remote_copy(
            src_ref=gbuf.at[slot, 1:3], dst_ref=gbuf.at[slot, 1:3],
            send_sem=gs_sem.at[o], recv_sem=gr_sem.at[slot],
            device_id={"shot": peer}, device_id_type=MESH)

    for o in range(1, shots):
        gather_copy(o, True).start()

    def field_down(which, source, dest, width, sending):
        return pltpu.make_async_remote_copy(
            src_ref=source.at[0, depth_len - width:depth_len],
            dst_ref=dest.at[halo - width:halo],
            send_sem=hs_sem.at[0, which], recv_sem=hr_sem.at[0, which],
            device_id={"depth": d + 1 if sending else d - 1}, device_id_type=MESH)

    def field_up(which, source, dest, width, sending):
        return pltpu.make_async_remote_copy(
            src_ref=source.at[0, 0:width],
            dst_ref=dest.at[halo + depth_len:halo + depth_len + width],
            send_sem=hs_sem.at[1, which], recv_sem=hr_sem.at[1, which],
            device_id={"depth": d - 1 if sending else d + 1}, device_id_type=MESH)

    both = ((0, last, field_a, halo), (1, late, field_b, reach))

    def model_down(slot, sending):
        return pltpu.make_async_remote_copy(
            src_ref=gbuf.at[slot, 2], dst_ref=gbuf.at[slot, 0],
            send_sem=fs_sem.at[0, slot], recv_sem=fr_sem.at[0, slot],
            device_id={"depth": d + 1 if sending else d - 1}, device_id_type=MESH)

    def model_up(slot, sending):
        return pltpu.make_async_remote_copy(
            src_ref=gbuf.at[slot, 1], dst_ref=gbuf.at[slot, 3],
            send_sem=fs_sem.at[1, slot], recv_sem=fr_sem.at[1, slot],
            device_id={"depth": d - 1 if sending else d + 1}, device_id_type=MESH)

    def spread(slot):
        @pl.when(has_down)
        def _():
            model_down(slot, True).start()

        @pl.when(has_up)
        def _():
            model_up(slot, True).start()

    spread(me)

    @pl.when(has_down)
    def _():
        for args in both:
            field_down(*args, True).start()

    @pl.when(has_up)
    def _():
        for args in both:
            field_up(*args, True).start()

    zeros_halo = jnp.zeros((halo, rows, cols), F32)

    @pl.when(jnp.logical_not(has_up))
    def _():
        field_a[0:halo] = zeros_halo
        field_b[0:halo] = zeros_halo

    @pl.when(jnp.logical_not(has_down))
    def _():
        field_a[halo + depth_len:] = zeros_halo
        field_b[halo + depth_len:] = zeros_halo

    field_a[halo:halo + depth_len] = last[0]
    field_b[halo:halo + depth_len] = late[0]

    shot = assignment[me]
    picked = []
    for k in range(3):
        chosen = jnp.zeros((1, receivers.shape[2]), jnp.int32)
        for j in range(receivers.shape[1]):
            chosen = chosen + jnp.where(shot == j, receivers[k, j:j + 1, :], 0)
        picked.append(chosen)
    place = (picked[0] - d * depth_len + reach) * rows + picked[1]
    count = receivers.shape[2]
    spot = lax.broadcasted_iota(jnp.int32, (window * rows, count), 0) == place
    spot = jnp.where(spot, 1.0, 0.0).astype(BF16)
    column = lax.broadcasted_iota(jnp.int32, (cols, count), 0) == picked[2]
    for i in range(steps):
        placed = jnp.where(column, residuals[0, i:i + 1, :], 0.0)
        inj[i] = split_dot(spot, placed, "values_right").reshape(window, rows, cols)

    for o in range(1, shots):
        gather_copy(o, False).wait_recv()
        spread(lax.rem(me + shots - o, shots))

    refine_y = jnp.zeros((2 * half_cols, 2 * cols), F32)
    c_in = lax.broadcasted_iota(jnp.int32, (2 * half_cols, 2 * cols), 0)
    f_out = lax.broadcasted_iota(jnp.int32, (2 * half_cols, 2 * cols), 1)
    same = (c_in >= half_cols) == (f_out >= cols)
    ci = jnp.where(c_in >= half_cols, c_in - half_cols, c_in)
    fo = jnp.where(f_out >= cols, f_out - cols, f_out)
    weight = jnp.where(fo == 2 * ci, 1.0, 0.0)
    weight = weight + jnp.where((fo == 2 * ci + 1) | (fo == 2 * ci - 1), 0.5, 0.0)
    weight = weight + jnp.where((fo == cols - 1) & (ci == half_cols - 1), 0.5, 0.0)
    refine_y = jnp.where(same, weight, 0.0).astype(BF16)

    @pl.when(has_up)
    def _():
        for slot in range(shots):
            model_down(slot, False).wait_recv()

    @pl.when(has_down)
    def _():
        for slot in range(shots):
            model_up(slot, False).wait_recv()

    pairs = 6 * rl
    for group in range(4):
        for s in range(shots):
            refined = split_dot(refine_y, gbuf[s, group], "values_left") * TIME_SQUARED
            for l2 in range(2):
                for c in range(3):
                    first = (l2 * 3 + c) * rl
                    piece = refined[first:first + rl]
                    coarse_y[c, 2 * group + l2, s * rl:(s + 1) * rl, :] = piece[:, 0:cols]
                    coarse_y[c + 3, 2 * group + l2, s * rl:(s + 1) * rl, :] = piece[:, cols:]

    row16 = lax.broadcasted_iota(jnp.int32, (coarse_rows, cols), 0)
    for c in range(6):
        scale = 1.0 if c < 3 else 0.25
        for l in range(2 * 4):
            here = coarse_y[c, l] * scale
            after = jnp.where(row16 == coarse_rows - 1, here, pltpu.roll(here, coarse_rows - 1, 0))
            fine_x[c, l, pl.ds(0, coarse_rows, stride=2), :] = here
            fine_x[c, l, pl.ds(1, coarse_rows, stride=2), :] = (here + after) * 0.5
    for c in range(6):
        for f in range(-reach, depth_len + reach):
            k = f // 2 + 2
            value = fine_x[c, k]
            if f % 2:
                after = fine_x[c, k + 1]
                if f == depth_len - 1:
                    after = jnp.where(has_down, after, value)
                value = (value + after) * 0.5
            if f < 0:
                value = jnp.where(has_up, value, 0.0)
            if f >= depth_len:
                value = jnp.where(has_down, value, 0.0)
            coef[c, f + reach] = value

    @pl.when(has_up)
    def _():
        for args in both:
            field_down(*args, False).wait_recv()

    @pl.when(has_down)
    def _():
        for args in both:
            field_up(*args, False).wait_recv()

    lane = lax.broadcasted_iota(jnp.int32, (rows, cols), 1)
    row = lax.broadcasted_iota(jnp.int32, (rows, cols), 0)
    lane_first, lane_last = lane == 0, lane == cols - 1
    row_first, row_last = row == 0, row == rows - 1

    def right(v):
        return jnp.where(lane_last, 0.0, pltpu.roll(v, cols - 1, 1))

    def left(v):
        return jnp.where(lane_first, 0.0, pltpu.roll(v, 1, 1))

    def under(v):
        return jnp.where(row_last, 0.0, pltpu.roll(v, rows - 1, 0))

    def over(v):
        return jnp.where(row_first, 0.0, pltpu.roll(v, 1, 0))

    def sides(v):
        xp, xm, yp, ym = under(v), over(v), right(v), left(v)
        return v, xp - xm, yp - ym, xp + xm, yp + ym

    source_z = sources[shot, 0] - d * depth_len
    source_x = sources[shot, 1]
    source_y = sources[shot, 2]
    mute_xy = (jnp.abs(row - source_x) <= MUTE) & (jnp.abs(lane - source_y) <= MUTE)

    current, previous = field_a, field_b
    for i in range(steps):
        extra = reach - i
        final = i == steps - 1

        def layer(f, before, here, after, owned, i=i, final=final, cur=current, prev=previous):
            v, dx, dy, sx, sy = here
            twice = 2.0 * v
            slopes = (
                after[0] - twice + before[0],
                sx - twice,
                sy - twice,
                after[1] - before[1],
                after[2] - before[2],
                under(dy) - over(dy),
            )
            acc = coef[0, f + reach] * slopes[0]
            for c in range(1, 6):
                acc = acc + coef[c, f + reach] * slopes[c]
            new = twice - prev[f + halo] + acc + inj[i, f + reach]
            if final:
                adjoint_first[0, f] = new
            else:
                prev[f + halo] = new
            if owned:
                wave = forward[i, 0, f].astype(F32)
                cross_wave = wave * 0.25
                for c in range(6):
                    term = (wave if c < 3 else cross_wave) * slopes[c]
                    if i:
                        term = totals[c, f] + term
                    if final:
                        hidden = mute_xy & (jnp.abs(f - source_z) <= MUTE)
                        term = jnp.where(hidden, 0.0, term)
                    totals[c, f] = term

        def run(first, stop, owned, carry, cur=current, layer=layer):
            def body(f, carry):
                before, here = carry
                after = sides(cur[f + 1 + halo])
                layer(f, before, here, after, owned)
                return here[:3], after
            return lax.fori_loop(first, stop, body, carry)

        carry = (sides(current[halo - extra - 1])[:3], sides(current[halo - extra]))
        if extra:
            carry = run(-extra, 0, False, carry)
        carry = run(0, depth_len, True, carry)
        if extra:
            carry = run(depth_len, depth_len + extra, False, carry)
        current, previous = previous, current

    fine_16 = lax.broadcasted_iota(jnp.int32, (coarse_rows, cols), 0)
    last_depth = jnp.where(has_down, 0.0, 0.5)
    for c in range(6):
        lanes = slice((c // 3) * cols, (c // 3) * cols + cols)
        for l in range(coarse_len + 1):
            if l == coarse_len:
                value = 0.5 * totals[c, depth_len - 1]
            else:
                value = totals[c, 2 * l] + 0.5 * totals[c, 2 * l + 1]
                if l:
                    value = value + 0.5 * totals[c, 2 * l - 1]
                if l == coarse_len - 1:
                    value = value + last_depth * totals[c, depth_len - 1]
            restr[c, l] = value
            even = restr[c, l, pl.ds(0, coarse_rows, stride=2), :]
            odd = restr[c, l, pl.ds(1, coarse_rows, stride=2), :]
            earlier = jnp.where(fine_16 == 0, 0.0, pltpu.roll(odd, 1, 0))
            tail = jnp.where(fine_16 == coarse_rows - 1, odd, 0.0)
            value = even + 0.5 * (odd + earlier + tail)
            for s in range(shots):
                piece = value[s * rl:(s + 1) * rl]
                if l == coarse_len:
                    lhs_rim[s, (c % 3) * rl:(c % 3 + 1) * rl, lanes] = piece
                else:
                    first = (l * 3 + c % 3) * rl
                    lhs_main[s, first:first + rl, lanes] = piece

    f_in = lax.broadcasted_iota(jnp.int32, (2 * cols, 2 * half_cols), 0)
    c_out = lax.broadcasted_iota(jnp.int32, (2 * cols, 2 * half_cols), 1)
    same = (f_in >= cols) == (c_out >= half_cols)
    fi = jnp.where(f_in >= cols, f_in - cols, f_in)
    co = jnp.where(c_out >= half_cols, c_out - half_cols, c_out)
    weight = jnp.where(fi == 2 * co, 1.0, 0.0)
    weight = weight + jnp.where((fi == 2 * co + 1) | (fi == 2 * co - 1), 0.5, 0.0)
    weight = weight + jnp.where((fi == cols - 1) & (co == half_cols - 1), 0.5, 0.0)
    coarsen_y = jnp.where(same, weight, 0.0).astype(BF16)
    main_rows, rim_rows = lhs_main.shape[1], lhs_rim.shape[1]
    outcome = split_dot(
        coarsen_y, lhs_main[...].reshape(shots * main_rows, 2 * cols), "values_left")
    send_main[...] = outcome.reshape(shots, main_rows, 2 * half_cols)
    outcome = split_dot(
        coarsen_y, lhs_rim[...].reshape(shots * rim_rows, 2 * cols), "values_left")
    send_rim[...] = outcome.reshape(shots, rim_rows, 2 * half_cols)

    def main_copy(o, sending):
        peer = lax.rem(me + o, shots) if sending else lax.rem(me + shots - o, shots)
        slot = me if sending else peer
        return pltpu.make_async_remote_copy(
            src_ref=send_main.at[peer], dst_ref=recv_main.at[slot],
            send_sem=ms_sem.at[o], recv_sem=mr_sem.at[slot],
            device_id={"shot": peer}, device_id_type=MESH)

    def rim_copy(o, sending):
        peer = lax.rem(me + o, shots) if sending else lax.rem(me + shots - o, shots)
        slot = me if sending else peer
        return pltpu.make_async_remote_copy(
            src_ref=send_rim.at[peer], dst_ref=recv_rim.at[slot],
            send_sem=rs_sem.at[o], recv_sem=rr_sem.at[slot],
            device_id={"depth": d + 1 if sending else d - 1, "shot": peer}, device_id_type=MESH)

    for o in range(1, shots):
        main_copy(o, True).start()

    @pl.when(has_down)
    def _():
        for o in range(shots):
            rim_copy(o, True).start()

    result = send_main[me]
    for o in range(1, shots):
        main_copy(o, False).wait_recv()
        result = result + recv_main[lax.rem(me + shots - o, shots)]
    total[0] = result

    @pl.when(has_up)
    def _():
        rim_sum = None
        for o in range(shots):
            rim_copy(o, False).wait_recv()
            piece = recv_rim[lax.rem(me + shots - o, shots)]
            rim_sum = piece if rim_sum is None else rim_sum + piece
        total[0, 0:3 * rl] = total[0, 0:3 * rl] + rim_sum[0:3 * rl]

    result = total[0] * (1.0 / steps)
    total[0] = result
    total[1] = pltpu.roll(result, half_cols, 1)
    for l in range(coarse_len):
        for c in range(3):
            first = (l * 3 + c) * rl
            gradients[c, l] = total[0, first:first + rl, 0:half_cols]
            gradients[c + 3, l] = total[1, first:first + rl, 0:half_cols]

    for o in range(1, shots):
        gather_copy(o, True).wait_send()
        main_copy(o, True).wait_send()

    @pl.when(has_down)
    def _():
        for args in both:
            field_down(*args, True).wait_send()
        for slot in range(shots):
            model_down(slot, True).wait_send()
        for o in range(shots):
            rim_copy(o, True).wait_send()

    @pl.when(has_up)
    def _():
        for args in both:
            field_up(*args, True).wait_send()
        for slot in range(shots):
            model_up(slot, True).wait_send()


def up8(n):
    return (n + 7) // 8 * 8


def on_device(
    forward, adjoint_last, adjoint_late, residuals, source_cells, receiver_cells, assignment, model
):
    steps, shots_here, depth_len, rows, cols = forward.shape
    channels, coarse_len, rl, half_cols = model.shape
    shots = lax.axis_size("shot")
    assert shots_here == 1 and coarse_len == 4 and steps == 4 and channels == 6
    window = depth_len + 2 * steps - 2
    coarse_rows = shots * rl
    field = (depth_len + 2 * steps, rows, cols)
    main_rows, rim_rows = up8(coarse_len * 3 * rl), up8(3 * rl)
    dma = pltpu.SemaphoreType.DMA
    vmem = pl.BlockSpec(memory_space=pltpu.VMEM)
    smem = pl.BlockSpec(memory_space=pltpu.SMEM)
    return pl.pallas_call(
        kernel,
        name="adjoint_gradient",
        out_shape=(
            jax.ShapeDtypeStruct(adjoint_last.shape, F32),
            jax.ShapeDtypeStruct(model.shape, F32),
        ),
        in_specs=[vmem] * 6 + [smem] * 2,
        out_specs=(vmem, vmem),
        scratch_shapes=[
            pltpu.VMEM((shots, 4, 6 * rl, 2 * half_cols), F32),
            pltpu.VMEM((6, 8, coarse_rows, cols), F32),
            pltpu.VMEM((6, 8, rows, cols), F32),
            pltpu.VMEM((6, window, rows, cols), F32),
            pltpu.VMEM(field, F32),
            pltpu.VMEM(field, F32),
            pltpu.VMEM((steps, window, rows, cols), F32),
            pltpu.VMEM((6, depth_len, rows, cols), F32),
            pltpu.VMEM((6, coarse_len + 1, rows, cols), F32),
            pltpu.VMEM((shots, main_rows, 2 * cols), F32),
            pltpu.VMEM((shots, rim_rows, 2 * cols), F32),
            pltpu.VMEM((shots, main_rows, 2 * half_cols), F32),
            pltpu.VMEM((shots, rim_rows, 2 * half_cols), F32),
            pltpu.VMEM((shots, main_rows, 2 * half_cols), F32),
            pltpu.VMEM((shots, rim_rows, 2 * half_cols), F32),
            pltpu.VMEM((2, main_rows, 2 * half_cols), F32),
            dma((shots,)), dma((shots,)),
            dma((2, 2)), dma((2, 2)),
            dma((2, shots)), dma((2, shots)),
            dma((shots,)), dma((shots,)),
            dma((shots,)), dma((shots,)),
        ],
        compiler_params=pltpu.CompilerParams(collective_id=0, has_side_effects=True),
    )(
        forward, adjoint_last, adjoint_late, residuals,
        jnp.transpose(receiver_cells, (2, 0, 1)), model, assignment, source_cells,
    )


def solution(mesh):
    placed = (
        P(None, ("grp", "shot"), "depth", None, None),
        P(("grp", "shot"), "depth", None, None),
        P(("grp", "shot"), "depth", None, None),
        P(("grp", "shot"), None, None),
        P("grp", None),
        P("grp", None, None),
        P("grp"),
        P(None, ("grp", "depth"), "shot", None),
    )
    return jax.shard_map(
        on_device,
        mesh=mesh,
        in_specs=placed,
        out_specs=(
            P(("grp", "shot"), "depth", None, None),
            P(None, ("grp", "depth"), "shot", None),
        ),
        check_vma=False,
    )
```

time: 178 us -> 25.2 us (0.14)
  the two profiles are of different devices: /device:TPU:0 before, /device:TPU:1 now
where the time goes in v1:
time: 25.2 us; the launch traced here: 25.1 us
  Pallas kernels  22.2 us (88%)
  local copies, waits for them, and re-layouts  2.2 us (9%)
  between operations  0.65 us (3%)
    pallas_call x1, Pallas kernels, on_device(): pl.pallas_call(kernel, name='adjoint_gradient', out_shape=(jax.ShapeDtype...  22.2 us
    unnamed x4, local copies, waits for them, and re-layouts  2.2 us

profile of v1, /device:TPU:1, one launch (start us, length us, event | category | flops | bytes accessed | tf_op | source)
XLA Modules:
  0.0 25.1 jit_solution(15917524420176420585)
XLA Ops:
  0.6 22.2 %adjoint_gradient.1 = (f32[1,8,32,128]{3,2,1,0:T(8,128)}, f32[6,4,4,64]{3,2,1,0:T(4,128)}) custom-call(bf16[4,1,8,32,128]{4,3,2,1,0:T(8,128)(2,1)} %forward.1, f32[1,8,32,128]{3,2,1,0:T(8,128)} %last.1, f32[1,8,32,128]{3,2,1,0:T(8,128)} %late.1, f32[1,4,256]{2,1,0:T(4,128)} %residuals.1, s32[3,4,256]{2,1,0:T(4,128)} %bitcast.1, f32[6,4,4,64]{3,2,1,0:T(4,128)} %model.1, ...), custom_call_target="tpu_custom_call" | custom-call | tf_op jit(solution)/shard_map/adjoint_gradient/pallas_call | solution.py:446
  22.8 0.0 copy-start
  22.8 1.6 %copy.12 = f32[1,8,32,128]{3,2,1,0:T(8,128)} copy(f32[1,8,32,128]{3,2,1,0:T(8,128)} %get-tuple-element.4) | data formatting | bytes 262144
  24.4 0.0 copy-done
  24.4 0.6 %copy.13 = f32[6,4,4,64]{3,2,1,0:T(4,128)} copy(f32[6,4,4,64]{3,2,1,0:T(4,128)S(1)} %copy-done) | data formatting | bytes 49152
Async XLA Ops:
  22.8 1.6 %copy-start = (f32[6,4,4,64]{3,2,1,0:T(4,128)S(1)}, f32[6,4,4,64]{3,2,1,0:T(4,128)}, u32[]{:S(2)}) copy-start(f32[6,4,4,64]{3,2,1,0:T(4,128)} %get-tuple-element.5) | copy-start | bytes 73732

commit v2 on v1

--- a/solution.py
+++ b/solution.py
@@ -27,11 +27,12 @@
 
 
 def kernel(
-    forward, last, late, residuals, receivers, model, assignment, sources,
-    adjoint_first, gradients,
+    forward_hbm, last_hbm, late_hbm, residuals_hbm, receivers_hbm, model_hbm, assignment, sources,
+    adjoint_hbm, gradients_hbm,
+    forward, last, late, residuals, receivers, model, adjoint_first, gradients,
     gbuf, coarse_y, fine_x, coef, field_a, field_b, inj, totals, restr, lhs_main, lhs_rim,
-    send_main, send_rim, recv_main, recv_rim, total,
-    gs_sem, gr_sem, hs_sem, hr_sem, fs_sem, fr_sem, ms_sem, mr_sem, rs_sem, rr_sem,
+    send_main, send_rim, recv_main, recv_rim, total, coarsen_ref,
+    gs_sem, gr_sem, hs_sem, hr_sem, fs_sem, fr_sem, ms_sem, mr_sem, rs_sem, rr_sem, in_sem, out_sem,
 ):
     steps = forward.shape[0]
     depth_len, rows, cols = last.shape[1:]
@@ -57,13 +58,21 @@
 
     @pl.when(has_up)
     def _():
-        for o in range(shots):
-            greet({"depth": d - 1, "shot": lax.rem(me + o, shots)})
+        greet({"depth": d - 1})
 
     @pl.when(has_down)
     def _():
-        for o in range(shots):
-            greet({"depth": d + 1, "shot": lax.rem(me + o, shots)})
+        greet({"depth": d + 1})
+
+    pulls = [
+        pltpu.make_async_copy(source, dest, in_sem.at[k])
+        for k, (source, dest) in enumerate((
+            (model_hbm, model), (last_hbm, last), (late_hbm, late), (receivers_hbm, receivers),
+            (residuals_hbm, residuals), (forward_hbm, forward)))
+    ]
+    for pull in pulls:
+        pull.start()
+    pulls[0].wait()
 
     for l in range(coarse_len):
         for c in range(3):
@@ -71,19 +80,24 @@
             first = ((l % 2) * 3 + c) * rl
             gbuf[me, 1 + l // 2, first:first + rl, :] = pair
 
-    beside = jnp.where(has_up, shots, 0) + jnp.where(has_down, shots, 0)
+    beside = jnp.where(has_up, 1, 0) + jnp.where(has_down, 1, 0)
     pl.semaphore_wait(barrier, shots - 1 + beside)
 
-    def gather_copy(o, sending):
-        peer = lax.rem(me + o, shots) if sending else lax.rem(me + shots - o, shots)
+    later = shots - 1 - me
+
+    def other(t):
+        return jnp.where(t < later, shots - 1 - t, t - later)
+
+    def gather_copy(t, sending):
+        peer = other(t)
         slot = me if sending else peer
         return pltpu.make_async_remote_copy(
             src_ref=gbuf.at[slot, 1:3], dst_ref=gbuf.at[slot, 1:3],
-            send_sem=gs_sem.at[o], recv_sem=gr_sem.at[slot],
+            send_sem=gs_sem.at[t], recv_sem=gr_sem.at[slot],
             device_id={"shot": peer}, device_id_type=MESH)
 
-    for o in range(1, shots):
-        gather_copy(o, True).start()
+    for t in range(shots - 1):
+        gather_copy(t, True).start()
 
     def field_down(which, source, dest, width, sending):
         return pltpu.make_async_remote_copy(
@@ -123,6 +137,8 @@
             model_up(slot, True).start()
 
     spread(me)
+    pulls[1].wait()
+    pulls[2].wait()
 
     @pl.when(has_down)
     def _():
@@ -149,6 +165,8 @@
     field_a[halo:halo + depth_len] = last[0]
     field_b[halo:halo + depth_len] = late[0]
 
+    pulls[3].wait()
+    pulls[4].wait()
     shot = assignment[me]
     picked = []
     for k in range(3):
@@ -165,11 +183,6 @@
         placed = jnp.where(column, residuals[0, i:i + 1, :], 0.0)
         inj[i] = split_dot(spot, placed, "values_right").reshape(window, rows, cols)
 
-    for o in range(1, shots):
-        gather_copy(o, False).wait_recv()
-        spread(lax.rem(me + shots - o, shots))
-
-    refine_y = jnp.zeros((2 * half_cols, 2 * cols), F32)
     c_in = lax.broadcasted_iota(jnp.int32, (2 * half_cols, 2 * cols), 0)
     f_out = lax.broadcasted_iota(jnp.int32, (2 * half_cols, 2 * cols), 1)
     same = (c_in >= half_cols) == (f_out >= cols)
@@ -180,18 +193,25 @@
     weight = weight + jnp.where((fo == cols - 1) & (ci == half_cols - 1), 0.5, 0.0)
     refine_y = jnp.where(same, weight, 0.0).astype(BF16)
 
-    @pl.when(has_up)
-    def _():
-        for slot in range(shots):
-            model_down(slot, False).wait_recv()
-
-    @pl.when(has_down)
-    def _():
-        for slot in range(shots):
-            model_up(slot, False).wait_recv()
-
-    pairs = 6 * rl
-    for group in range(4):
+    f_in = lax.broadcasted_iota(jnp.int32, (2 * cols, 2 * half_cols), 0)
+    c_out = lax.broadcasted_iota(jnp.int32, (2 * cols, 2 * half_cols), 1)
+    same = (f_in >= cols) == (c_out >= half_cols)
+    fi = jnp.where(f_in >= cols, f_in - cols, f_in)
+    co = jnp.where(c_out >= half_cols, c_out - half_cols, c_out)
+    weight = jnp.where(fi == 2 * co, 1.0, 0.0)
+    weight = weight + jnp.where((fi == 2 * co + 1) | (fi == 2 * co - 1), 0.5, 0.0)
+    weight = weight + jnp.where((fi == cols - 1) & (co == half_cols - 1), 0.5, 0.0)
+    coarsen_y = jnp.where(same, weight, 0.0).astype(BF16)
+    coarsen_ref[...] = coarsen_y
+
+    pulls[5].wait()
+    for t in range(shots - 1):
+        gather_copy(t, False).wait_recv()
+        spread(other(t))
+
+    row16 = lax.broadcasted_iota(jnp.int32, (coarse_rows, cols), 0)
+
+    def refine_group(group):
         for s in range(shots):
             refined = split_dot(refine_y, gbuf[s, group], "values_left") * TIME_SQUARED
             for l2 in range(2):
@@ -200,29 +220,49 @@
                     piece = refined[first:first + rl]
                     coarse_y[c, 2 * group + l2, s * rl:(s + 1) * rl, :] = piece[:, 0:cols]
                     coarse_y[c + 3, 2 * group + l2, s * rl:(s + 1) * rl, :] = piece[:, cols:]
-
-    row16 = lax.broadcasted_iota(jnp.int32, (coarse_rows, cols), 0)
-    for c in range(6):
-        scale = 1.0 if c < 3 else 0.25
-        for l in range(2 * 4):
-            here = coarse_y[c, l] * scale
-            after = jnp.where(row16 == coarse_rows - 1, here, pltpu.roll(here, coarse_rows - 1, 0))
-            fine_x[c, l, pl.ds(0, coarse_rows, stride=2), :] = here
-            fine_x[c, l, pl.ds(1, coarse_rows, stride=2), :] = (here + after) * 0.5
-    for c in range(6):
-        for f in range(-reach, depth_len + reach):
-            k = f // 2 + 2
-            value = fine_x[c, k]
-            if f % 2:
-                after = fine_x[c, k + 1]
-                if f == depth_len - 1:
-                    after = jnp.where(has_down, after, value)
-                value = (value + after) * 0.5
-            if f < 0:
-                value = jnp.where(has_up, value, 0.0)
-            if f >= depth_len:
-                value = jnp.where(has_down, value, 0.0)
-            coef[c, f + reach] = value
+        for c in range(6):
+            scale = 1.0 if c < 3 else 0.25
+            for l in (2 * group, 2 * group + 1):
+                here = coarse_y[c, l] * scale
+                after = pltpu.roll(here, coarse_rows - 1, 0)
+                after = jnp.where(row16 == coarse_rows - 1, here, after)
+                fine_x[c, l, pl.ds(0, coarse_rows, stride=2), :] = here
+                fine_x[c, l, pl.ds(1, coarse_rows, stride=2), :] = (here + after) * 0.5
+
+    def refine_depth(first, stop):
+        for c in range(6):
+            for f in range(first, stop):
+                k = f // 2 + 2
+                value = fine_x[c, k]
+                if f % 2:
+                    after = fine_x[c, k + 1]
+                    if f == depth_len - 1:
+                        after = jnp.where(has_down, after, value)
+                    value = (value + after) * 0.5
+                if f < 0:
+                    value = jnp.where(has_up, value, 0.0)
+                if f >= depth_len:
+                    value = jnp.where(has_down, value, 0.0)
+                coef[c, f + reach] = value
+
+    refine_group(1)
+    refine_group(2)
+    refine_depth(0, depth_len - 1)
+
+    @pl.when(has_up)
+    def _():
+        for slot in range(shots):
+            model_down(slot, False).wait_recv()
+
+    @pl.when(has_down)
+    def _():
+        for slot in range(shots):
+            model_up(slot, False).wait_recv()
+
+    refine_group(0)
+    refine_group(3)
+    refine_depth(-reach, 0)
+    refine_depth(depth_len - 1, depth_len + reach)
 
     @pl.when(has_up)
     def _():
@@ -312,6 +352,9 @@
             carry = run(depth_len, depth_len + extra, False, carry)
         current, previous = previous, current
 
+    push_field = pltpu.make_async_copy(adjoint_first, adjoint_hbm, out_sem.at[0])
+    push_field.start()
+
     fine_16 = lax.broadcasted_iota(jnp.int32, (coarse_rows, cols), 0)
     last_depth = jnp.where(has_down, 0.0, 0.5)
     for c in range(6):
@@ -339,29 +382,20 @@
                     first = (l * 3 + c % 3) * rl
                     lhs_main[s, first:first + rl, lanes] = piece
 
-    f_in = lax.broadcasted_iota(jnp.int32, (2 * cols, 2 * half_cols), 0)
-    c_out = lax.broadcasted_iota(jnp.int32, (2 * cols, 2 * half_cols), 1)
-    same = (f_in >= cols) == (c_out >= half_cols)
-    fi = jnp.where(f_in >= cols, f_in - cols, f_in)
-    co = jnp.where(c_out >= half_cols, c_out - half_cols, c_out)
-    weight = jnp.where(fi == 2 * co, 1.0, 0.0)
-    weight = weight + jnp.where((fi == 2 * co + 1) | (fi == 2 * co - 1), 0.5, 0.0)
-    weight = weight + jnp.where((fi == cols - 1) & (co == half_cols - 1), 0.5, 0.0)
-    coarsen_y = jnp.where(same, weight, 0.0).astype(BF16)
     main_rows, rim_rows = lhs_main.shape[1], lhs_rim.shape[1]
     outcome = split_dot(
-        coarsen_y, lhs_main[...].reshape(shots * main_rows, 2 * cols), "values_left")
+        coarsen_ref[...], lhs_main[...].reshape(shots * main_rows, 2 * cols), "values_left")
     send_main[...] = outcome.reshape(shots, main_rows, 2 * half_cols)
     outcome = split_dot(
-        coarsen_y, lhs_rim[...].reshape(shots * rim_rows, 2 * cols), "values_left")
+        coarsen_ref[...], lhs_rim[...].reshape(shots * rim_rows, 2 * cols), "values_left")
     send_rim[...] = outcome.reshape(shots, rim_rows, 2 * half_cols)
 
-    def main_copy(o, sending):
-        peer = lax.rem(me + o, shots) if sending else lax.rem(me + shots - o, shots)
+    def main_copy(t, sending):
+        peer = other(t)
         slot = me if sending else peer
         return pltpu.make_async_remote_copy(
             src_ref=send_main.at[peer], dst_ref=recv_main.at[slot],
-            send_sem=ms_sem.at[o], recv_sem=mr_sem.at[slot],
+            send_sem=ms_sem.at[t], recv_sem=mr_sem.at[slot],
             device_id={"shot": peer}, device_id_type=MESH)
 
     def rim_copy(o, sending):
@@ -372,8 +406,8 @@
             send_sem=rs_sem.at[o], recv_sem=rr_sem.at[slot],
             device_id={"depth": d + 1 if sending else d - 1, "shot": peer}, device_id_type=MESH)
 
-    for o in range(1, shots):
-        main_copy(o, True).start()
+    for t in range(shots - 1):
+        main_copy(t, True).start()
 
     @pl.when(has_down)
     def _():
@@ -381,9 +415,9 @@
             rim_copy(o, True).start()
 
     result = send_main[me]
-    for o in range(1, shots):
-        main_copy(o, False).wait_recv()
-        result = result + recv_main[lax.rem(me + shots - o, shots)]
+    for t in range(shots - 1):
+        main_copy(t, False).wait_recv()
+        result = result + recv_main[other(t)]
     total[0] = result
 
     @pl.when(has_up)
@@ -404,9 +438,12 @@
             gradients[c, l] = total[0, first:first + rl, 0:half_cols]
             gradients[c + 3, l] = total[1, first:first + rl, 0:half_cols]
 
-    for o in range(1, shots):
-        gather_copy(o, True).wait_send()
-        main_copy(o, True).wait_send()
+    push_gradients = pltpu.make_async_copy(gradients, gradients_hbm, out_sem.at[1])
+    push_gradients.start()
+
+    for t in range(shots - 1):
+        gather_copy(t, True).wait_send()
+        main_copy(t, True).wait_send()
 
     @pl.when(has_down)
     def _():
@@ -423,6 +460,9 @@
             field_up(*args, True).wait_send()
         for slot in range(shots):
             model_up(slot, True).wait_send()
+
+    push_field.wait()
+    push_gradients.wait()
 
 
 def up8(n):
@@ -441,7 +481,9 @@
     field = (depth_len + 2 * steps, rows, cols)
     main_rows, rim_rows = up8(coarse_len * 3 * rl), up8(3 * rl)
     dma = pltpu.SemaphoreType.DMA
-    vmem = pl.BlockSpec(memory_space=pltpu.VMEM)
+    hbm = pl.BlockSpec(memory_space=pltpu.HBM)
+    anywhere = pl.BlockSpec(memory_space=pl.ANY)
+    receivers = jnp.transpose(receiver_cells, (2, 0, 1))
     smem = pl.BlockSpec(memory_space=pltpu.SMEM)
     return pl.pallas_call(
         kernel,
@@ -450,9 +492,17 @@
             jax.ShapeDtypeStruct(adjoint_last.shape, F32),
             jax.ShapeDtypeStruct(model.shape, F32),
         ),
-        in_specs=[vmem] * 6 + [smem] * 2,
-        out_specs=(vmem, vmem),
+        in_specs=[hbm] * 6 + [smem] * 2,
+        out_specs=(anywhere, anywhere),
         scratch_shapes=[
+            pltpu.VMEM(forward.shape, forward.dtype),
+            pltpu.VMEM(adjoint_last.shape, F32),
+            pltpu.VMEM(adjoint_late.shape, F32),
+            pltpu.VMEM(residuals.shape, F32),
+            pltpu.VMEM(receivers.shape, receivers.dtype),
+            pltpu.VMEM(model.shape, F32),
+            pltpu.VMEM(adjoint_last.shape, F32),
+            pltpu.VMEM(model.shape, F32),
             pltpu.VMEM((shots, 4, 6 * rl, 2 * half_cols), F32),
             pltpu.VMEM((6, 8, coarse_rows, cols), F32),
             pltpu.VMEM((6, 8, rows, cols), F32),
@@ -469,16 +519,19 @@
             pltpu.VMEM((shots, main_rows, 2 * half_cols), F32),
             pltpu.VMEM((shots, rim_rows, 2 * half_cols), F32),
             pltpu.VMEM((2, main_rows, 2 * half_cols), F32),
+            pltpu.VMEM((2 * cols, 2 * half_cols), BF16),
             dma((shots,)), dma((shots,)),
             dma((2, 2)), dma((2, 2)),
             dma((2, shots)), dma((2, shots)),
             dma((shots,)), dma((shots,)),
             dma((shots,)), dma((shots,)),
+            dma((6,)), dma((2,)),
         ],
-        compiler_params=pltpu.CompilerParams(collective_id=0, has_side_effects=True),
+        compiler_params=pltpu.CompilerParams(
+            collective_id=0, has_side_effects=True),
     )(
         forward, adjoint_last, adjoint_late, residuals,
-        jnp.transpose(receiver_cells, (2, 0, 1)), model, assignment, source_cells,
+        receivers, model, assignment, source_cells,
     )
 
 

time: 25.2 us -> 24.1 us (0.956)
  Pallas kernels: 22.2 us -> 21 us
    pallas_call x1, Pallas kernels: 22.2 us -> 21 us  [on_device(): pl.pallas_call(kernel, name='adjoint_gradient', out_shape=(jax.ShapeDtype...]
where the time goes in v2:
time: 24.1 us; the launch traced here: 23.9 us
  Pallas kernels  21 us (87%)
  local copies, waits for them, and re-layouts  2.2 us (9%)
  between operations  0.65 us (3%)
    pallas_call x1, Pallas kernels, on_device(): pl.pallas_call(kernel, name='adjoint_gradient', out_shape=(jax.ShapeDtype...  21 us
    unnamed x4, local copies, waits for them, and re-layouts  2.2 us

profile of v2, /device:TPU:1, one launch (start us, length us, event | category | flops | bytes accessed | tf_op | source)
XLA Modules:
  0.0 23.9 jit_solution(15048853839425934305)
XLA Ops:
  0.6 21.0 %adjoint_gradient.1 = (f32[1,8,32,128]{3,2,1,0:T(8,128)}, f32[6,4,4,64]{3,2,1,0:T(4,128)}) custom-call(bf16[4,1,8,32,128]{4,3,2,1,0:T(8,128)(2,1)} %forward_hbm.1, f32[1,8,32,128]{3,2,1,0:T(8,128)} %last_hbm.1, f32[1,8,32,128]{3,2,1,0:T(8,128)} %late_hbm.1, f32[1,4,256]{2,1,0:T(4,128)} %residuals_hbm.1, s32[3,4,256]{2,1,0:T(4,128)} %bitcast.1, ...), custom_call_target="tpu_custom_call" | custom-call | tf_op jit(solution)/shard_map/adjoint_gradient/pallas_call | solution.py:488
  21.7 0.0 copy-start
  21.7 1.6 %copy.12 = f32[1,8,32,128]{3,2,1,0:T(8,128)} copy(f32[1,8,32,128]{3,2,1,0:T(8,128)} %get-tuple-element.4) | data formatting | bytes 262144
  23.3 0.0 copy-done
  23.3 0.6 %copy.13 = f32[6,4,4,64]{3,2,1,0:T(4,128)} copy(f32[6,4,4,64]{3,2,1,0:T(4,128)S(1)} %copy-done) | data formatting | bytes 49152
Async XLA Ops:
  21.7 1.6 %copy-start = (f32[6,4,4,64]{3,2,1,0:T(4,128)S(1)}, f32[6,4,4,64]{3,2,1,0:T(4,128)}, u32[]{:S(2)}) copy-start(f32[6,4,4,64]{3,2,1,0:T(4,128)} %get-tuple-element.5) | copy-start | bytes 73732

commit v3 on v2

--- a/solution.py
+++ b/solution.py
@@ -181,7 +181,10 @@
     column = lax.broadcasted_iota(jnp.int32, (cols, count), 0) == picked[2]
     for i in range(steps):
         placed = jnp.where(column, residuals[0, i:i + 1, :], 0.0)
-        inj[i] = split_dot(spot, placed, "values_right").reshape(window, rows, cols)
+        high = placed.astype(BF16)
+        low = (placed - high.astype(F32)).astype(BF16)
+        both_parts = exact_dot(spot, jnp.concatenate([high, low], axis=0), "values_right")
+        inj[i] = (both_parts[:, 0:cols] + both_parts[:, cols:]).reshape(window, rows, cols)
 
     c_in = lax.broadcasted_iota(jnp.int32, (2 * half_cols, 2 * cols), 0)
     f_out = lax.broadcasted_iota(jnp.int32, (2 * half_cols, 2 * cols), 1)
@@ -212,8 +215,16 @@
     row16 = lax.broadcasted_iota(jnp.int32, (coarse_rows, cols), 0)
 
     def refine_group(group):
+        width = 6 * rl
+        merged = width % 8 == 0
+        if merged:
+            slab = gbuf[:, group].reshape(shots * width, 2 * half_cols)
+            slab = split_dot(refine_y, slab, "values_left") * TIME_SQUARED
         for s in range(shots):
-            refined = split_dot(refine_y, gbuf[s, group], "values_left") * TIME_SQUARED
+            if merged:
+                refined = slab[s * width:(s + 1) * width]
+            else:
+                refined = split_dot(refine_y, gbuf[s, group], "values_left") * TIME_SQUARED
             for l2 in range(2):
                 for c in range(3):
                     first = (l2 * 3 + c) * rl
@@ -337,12 +348,12 @@
                     totals[c, f] = term
 
         def run(first, stop, owned, carry, cur=current, layer=layer):
-            def body(f, carry):
-                before, here = carry
+            before, here = carry
+            for f in range(first, stop):
                 after = sides(cur[f + 1 + halo])
                 layer(f, before, here, after, owned)
-                return here[:3], after
-            return lax.fori_loop(first, stop, body, carry)
+                before, here = here[:3], after
+            return before, here
 
         carry = (sides(current[halo - extra - 1])[:3], sides(current[halo - extra]))
         if extra:

time: 24.1 us -> 21.3 us (0.88)
  Pallas kernels: 21 us -> 18.3 us
    pallas_call x1, Pallas kernels: 21 us -> 18.3 us  [on_device(): pl.pallas_call(kernel, name='adjoint_gradient', out_shape=(jax.ShapeDtype...]
where the time goes in v3:
time: 21.3 us; the launch traced here: 21.1 us
  Pallas kernels  18.3 us (86%)
  local copies, waits for them, and re-layouts  2.2 us (10%)
  between operations  0.65 us (3%)
    pallas_call x1, Pallas kernels, on_device(): pl.pallas_call(kernel, name='adjoint_gradient', out_shape=(jax.ShapeDtype...  18.3 us
    unnamed x4, local copies, waits for them, and re-layouts  2.2 us

profile of v3, /device:TPU:1, one launch (start us, length us, event | category | flops | bytes accessed | tf_op | source)
XLA Modules:
  0.0 21.1 jit_solution(3134594581775628512)
XLA Ops:
  0.6 18.3 %adjoint_gradient.1 = (f32[1,8,32,128]{3,2,1,0:T(8,128)}, f32[6,4,4,64]{3,2,1,0:T(4,128)}) custom-call(bf16[4,1,8,32,128]{4,3,2,1,0:T(8,128)(2,1)} %forward_hbm.1, f32[1,8,32,128]{3,2,1,0:T(8,128)} %last_hbm.1, f32[1,8,32,128]{3,2,1,0:T(8,128)} %late_hbm.1, f32[1,4,256]{2,1,0:T(4,128)} %residuals_hbm.1, s32[3,4,256]{2,1,0:T(4,128)} %bitcast.1, ...), custom_call_target="tpu_custom_call" | custom-call | tf_op jit(solution)/shard_map/adjoint_gradient/pallas_call | solution.py:499
  18.9 0.0 copy-start
  18.9 1.6 %copy.12 = f32[1,8,32,128]{3,2,1,0:T(8,128)} copy(f32[1,8,32,128]{3,2,1,0:T(8,128)} %get-tuple-element.4) | data formatting | bytes 262144
  20.5 0.0 copy-done
  20.5 0.6 %copy.13 = f32[6,4,4,64]{3,2,1,0:T(4,128)} copy(f32[6,4,4,64]{3,2,1,0:T(4,128)S(1)} %copy-done) | data formatting | bytes 49152
Async XLA Ops:
  18.9 1.6 %copy-start = (f32[6,4,4,64]{3,2,1,0:T(4,128)S(1)}, f32[6,4,4,64]{3,2,1,0:T(4,128)}, u32[]{:S(2)}) copy-start(f32[6,4,4,64]{3,2,1,0:T(4,128)} %get-tuple-element.5) | copy-start | bytes 73732
